TPU v7x, 32 devices: a whole 2x2x4 slice. The times are simulated.
32 devices in a mesh: grp: 2 (over y), tgt: 4 (over z), src: 4 (over x, core).
Axes of the slice: x: 2, y: 2, z: 4, core: 2. Of those that a mesh axis runs over, the one named last changes fastest.
Arguments:
- target_rows: bfloat16 [2048, 4608], P(('grp', 'tgt', 'src')), parts along dimension 0, may hold values from -6 to 6
- target_pos: int32 [2048], P(('grp', 'tgt')), parts along dimension 0, may hold values from 0 to 255
- decoder_rows: bfloat16 [512, 4608], P(('grp', 'tgt', 'src')), parts along dimension 0, may hold values from -0.09375 to 0.09375
- source_pos: int32 [512], P('grp'), parts along dimension 0, may hold values from 0 to 255
- out_proj: bfloat16 [32, 4608, 128], P('src', 'tgt'), may hold values from -0.09375 to 0.09375
- value_proj: bfloat16 [16, 4608, 128], P('src'), may hold values from -1 to 1
- attention: bfloat16 [64, 256, 256], P(('grp', 'src'), 'tgt'), parts along dimension 0, may hold values from 0 to 1, as said below
- tile_pattern: int32 [8, 4], P('grp'), parts along dimension 0, may hold values from 0 to 1, as said below
Outputs:
- edges: bfloat16 [512, 1024], P(('grp', 'src'), 'tgt'), parts along dimension 0
There are 2 independent parts, one for each index of `grp`. A program takes and returns all parts, laid end to end along the dimension named above; an argument that names none is the same for every part. Nothing has to cross between parts.
Inputs may be any that keep to these rules, and one draw needn't show every extreme that they name: Each row attention[h, p, :] is a probability distribution over the keys 0 to p: zero beyond p, summing to one. tile_pattern[b, c] is 1 where the tile of edges between source block b and target block c is kept, else 0.
All inputs are finite; a program needn't handle non-finite values.
Results may differ from a plain program's by a relative error of at most 0.0057.
Values may be sent and summed in bfloat16 or wider, within the bound.
A program may use at most 64 MiB of HBM per device.

v0:
```python
import jax
import jax.numpy as jnp
from jax import lax
from jax.sharding import PartitionSpec as P


def passed_along(value, axis, steps):
    count = lax.axis_size(axis)
    pairs = [(source, (source + steps) % count) for source in range(count)]
    return lax.ppermute(value, axis, pairs)


def shards(
    target_rows, target_pos, decoder_rows, source_pos, out_proj, value_proj, attention, tile_pattern
):
    blocks = lax.axis_size("tgt")
    column = lax.axis_index("tgt")
    src_lane = lax.axis_index("src")
    full_targets, full_sources = (
        lax.all_gather(target_rows, "src", axis=0, tiled=True),
        lax.all_gather(decoder_rows, "src", axis=0, tiled=True),
    )
    tgt_dev = full_targets.shape[0]
    src_dev = full_sources.shape[0]
    sub_rows = decoder_rows.shape[0]
    heads_here = out_proj.shape[0]
    head_dim = out_proj.shape[2]
    groups_here = value_proj.shape[0]
    repeat = heads_here // groups_here
    read_sum = jnp.einsum(
        "td,hde->the",
        full_targets,
        lax.all_gather(out_proj, "tgt", axis=1, tiled=True),
        preferred_element_type=jnp.float32,
    )
    head_reads = read_sum.astype(jnp.bfloat16).reshape(tgt_dev, groups_here, repeat, head_dim)
    values = jnp.einsum("sd,gde->sge", full_sources, value_proj, preferred_element_type=jnp.float32)
    values = values.astype(jnp.bfloat16).reshape(src_dev, groups_here * head_dim)
    attn_table = lax.all_gather(attention, "tgt", axis=1, tiled=True)
    target_attn = jnp.take(attn_table, target_pos, axis=1)
    keyed_attn = jnp.transpose(target_attn, (0, 2, 1))

    def edge_tile(payload, block_index):
        decoder_part, value_part = payload
        key_positions = lax.dynamic_slice_in_dim(source_pos, block_index * src_dev, src_dev)
        weights = jnp.take(keyed_attn, key_positions, axis=1).astype(jnp.float32)
        scores = jnp.einsum(
            "sgd,tgrd->grst",
            value_part.reshape(src_dev, groups_here, head_dim),
            head_reads,
            preferred_element_type=jnp.float32,
        )
        scores = scores.reshape(heads_here, src_dev, tgt_dev)
        mixed_term = jnp.sum(weights * scores, axis=0)
        own_positions = lax.dynamic_slice_in_dim(key_positions, src_lane * sub_rows, sub_rows)
        same_place = (own_positions[:, None] == target_pos[None, :]).astype(jnp.float32)
        direct = (
            jnp.einsum("sd,td->st", decoder_part, full_targets, preferred_element_type=jnp.float32)
            * same_place
        )
        own_rows = lax.dynamic_slice_in_dim(mixed_term, src_lane * sub_rows, sub_rows, 0)
        return lax.dynamic_update_slice_in_dim(
            mixed_term, own_rows + direct, src_lane * sub_rows, 0
        )

    def place_tile(partial_value, payload, block_index):
        kept_flag = tile_pattern[block_index, column]
        piece_tile = edge_tile(payload, block_index) * kept_flag.astype(jnp.float32)
        return lax.dynamic_update_slice_in_dim(partial_value, piece_tile, block_index * src_dev, 0)

    own_block = (decoder_rows, values)
    partial_value = jnp.zeros((blocks * src_dev, tgt_dev), jnp.float32)
    partial_value = place_tile(partial_value, own_block, column)

    def cycle_turn(turn_index, state_carry):
        forward_block, backward_block, running = state_carry
        forward_block = passed_along((forward_block[0], forward_block[1]), "tgt", 1)
        backward_block = passed_along((backward_block[0], backward_block[1]), "tgt", -1)
        running = place_tile(running, forward_block, (column - turn_index) % blocks)
        running = place_tile(running, backward_block, (column + turn_index) % blocks)
        return (forward_block, backward_block, running)

    forward_block, backward_block, partial_value = lax.fori_loop(
        1, blocks // 2, cycle_turn, (own_block, own_block, partial_value)
    )
    forward_block = passed_along((forward_block[0], forward_block[1]), "tgt", 1)
    partial_value = place_tile(partial_value, forward_block, (column - blocks // 2) % blocks)
    summed = lax.psum_scatter(partial_value, "src", scatter_dimension=0, tiled=True)
    return summed.astype(jnp.bfloat16)


def solution(mesh):
    return jax.shard_map(
        shards,
        mesh=mesh,
        in_specs=(
            P(("grp", "tgt", "src"), None),
            P(("grp", "tgt")),
            P(("grp", "tgt", "src"), None),
            P("grp"),
            P("src", "tgt", None),
            P("src", None, None),
            P(("grp", "src"), "tgt", None),
            P("grp", None),
        ),
        out_specs=P(("grp", "src"), "tgt"),
        check_vma=False,
    )
```

profile of v0, /device:TPU:0, one launch (start us, length us, event | category | flops | bytes accessed | tf_op | source)
XLA Modules:
  0.0 277.3 jit_solution(18094460157816442848)
XLA Ops:
  6.5 1.9 copy.26
  8.4 0.0 all-gather.4.cloned.1.call-update
  8.4 0.0 all-gather.6.cloned.1.call-start
  8.5 0.7 all-gather.6.cloned.1.call-update
  9.2 0.0 all-gather.8.cloned.1.call-start
  9.2 0.7 all-gather.8.cloned.1.call-update
  9.9 0.0 reduce-scatter.2.cloned.1.call-start
  10.0 5.1 %collective-permute-start.3 = (bf16[16,4608]{1,0:T(8,128)(2,1)S(1)}, bf16[16,4608]{1,0:T(8,128)(2,1)S(1)}, u32[]{:S(2)}, u32[]{:S(2)}) collective-permute-start(bf16[16,4608]{1,0:T(8,128)(2,1)S(1)} %copy-done.2), channel_id=1, source_target_pairs={{0,12},{4,0},{8,4},{12,8},{1,13},{5,1},{9,5},{13,9},{2,14},{6,2},{... | collective-permute-start | bytes 442376 | tf_op jit(solution)/shard_map/while/body/eval_jaxpr/ppermute | solution.py:10
  15.1 0.0 collective-permute-start.1
  15.1 7.5 %all_gather.15 = bf16[64,4608]{1,0:T(8,128)(2,1)S(1)} all-gather(bf16[16,4608]{1,0:T(8,128)(2,1)S(1)} %copy-done.2), channel_id=1, replica_groups=mesh['grp'=2,'tgt'=4,'src'=4] {'src'}, dimensions={0}, use_global_device_ids=true | all-gather | bytes 737280 | tf_op jit(solution)/shard_map/all_gather | solution.py:21
  22.6 3.3 %convolution_convert_fusion = bf16[64,4,128]{2,0,1:T(8,128)(2,1)S(1)} fusion(bf16[4,4608,128]{2,1,0:T(8,128)(2,1)} %param.15, bf16[64,4608]{1,0:T(8,128)(2,1)S(1)} %all_gather.15), kind=kOutput, calls=%fused_computation.8 | convolution fusion | flops 302022656 | bytes 5373952 | tf_op jit(solution)/shard_map/sd,gde->sge/dot_general | solution.py:37
  26.0 3.9 %collective-permute-start.2 = (bf16[64,512]{1,0:T(8,128)(2,1)S(1)}, bf16[64,512]{1,0:T(8,128)(2,1)S(1)}, u32[]{:S(2)}, u32[]{:S(2)}) collective-permute-start(bf16[64,512]{1,0:T(8,128)(2,1)S(1)} %copy_bitcast_fusion), channel_id=1, source_target_pairs={{0,12},{4,0},{8,4},{12,8},{1,13},{5,1},{9,5},{13,9},{2,14},{6,2},{... | collective-permute-start | bytes 196616 | tf_op jit(solution)/shard_map/while/body/eval_jaxpr/ppermute | solution.py:10
  29.8 0.0 collective-permute-start
  29.9 0.1 compare_and_fusion
  30.1 0.7 fusion.26
  33.4 4.4 %collective-permute-done = bf16[64,512]{1,0:T(8,128)(2,1)S(1)} collective-permute-done((bf16[64,512]{1,0:T(8,128)(2,1)S(1)}, bf16[64,512]{1,0:T(8,128)(2,1)S(1)}, u32[]{:S(2)}, u32[]{:S(2)}) %collective-permute-start) | collective-permute-done | bytes 65568 | tf_op jit(solution)/shard_map/while/body/eval_jaxpr/ppermute | solution.py:10
  37.8 1.1 collective-permute-start.4
  38.9 0.1 fusion.27
  39.0 0.0 collective-permute-done.2
  39.0 5.8 %collective-permute-done.4 = bf16[64,512]{1,0:T(8,128)(2,1)S(1)} collective-permute-done((bf16[64,512]{1,0:T(8,128)(2,1)S(1)}, bf16[64,512]{1,0:T(8,128)(2,1)S(1)}, u32[]{:S(2)}, u32[]{:S(2)}) %collective-permute-start.4) | collective-permute-done | bytes 65568 | tf_op jit(solution)/shard_map/ppermute | solution.py:10
  44.8 0.0 collective-permute-done.1
  44.8 0.1 collective-permute-start.5
  44.9 2.0 gather_fusion
  46.9 0.9 select_bitcast_fusion
  47.8 1.3 copy.27
  49.1 0.6 gather_fusion.4
  49.7 0.6 gather_fusion.3
  50.3 0.6 gather_fusion.2
  50.9 0.6 gather_fusion.1
  51.5 17.4 %all-gather.6.cloned.1.call-done = bf16[256,4608]{1,0:T(8,128)(2,1)} async-done(((bf16[64,4608]{1,0:T(8,128)(2,1)}), bf16[256,4608]{1,0:T(8,128)(2,1)}) %all-gather.6.cloned.1.call-update) | async-done | bytes 2359312 | tf_op jit(solution)/shard_map/all_gather | solution.py:20
  68.9 168.4 %all-gather.8.cloned.1.call-done = bf16[8,4608,128]{2,1,0:T(8,128)(2,1)} async-done(((bf16[8,1152,128]{2,1,0:T(8,128)(2,1)}), bf16[8,4608,128]{2,1,0:T(8,128)(2,1)}) %all-gather.8.cloned.1.call-update) | async-done | bytes 9437200 | tf_op jit(solution)/shard_map/all_gather | solution.py:33
  237.2 7.0 %fusion.2 = bf16[256,8,128]{2,0,1:T(8,128)(2,1)S(1)} fusion(bf16[8,4608,128]{2,1,0:T(8,128)(2,1)} %all-gather.8.cloned.1.call-done, bf16[256,4608]{1,0:T(8,128)(2,1)} %all-gather.6.cloned.1.call-done), kind=kOutput, calls=%fused_computation.7 | convolution fusion | flops 2416181248 | bytes 12320768 | tf_op jit(solution)/shard_map/td,hde->the/dot_general | solution.py:30
  244.2 0.3 fusion.18
  244.5 0.3 fusion.20
  244.8 0.3 fusion.24
  245.1 0.3 fusion.22
  245.5 0.4 fusion.16
  245.9 0.4 fusion.17
  246.3 0.7 fusion.12
  247.1 0.7 fusion.10
  247.9 0.4 fusion.15
  248.3 0.7 fusion.8
  249.1 0.4 fusion.14
  249.5 0.7 fusion.6
  250.3 0.7 copy-done.1
  250.9 0.0 reduce-scatter.2.cloned.1.call-update
  251.0 18.4 %reduce-scatter.2.cloned.1.call-done = f32[64,256]{1,0:T(8,128)} async-done(((f32[256,256]{1,0:T(8,128)}), f32[64,256]{1,0:T(8,128)}) %reduce-scatter.2.cloned.1.call-update) | async-done | bytes 65552 | tf_op jit(solution)/shard_map/reduce_scatter | solution.py:88
  269.3 1.5 convert_element_type.69
  (30 shorter events, 0.3 us)
Async XLA Ops:
  6.5 3.4 %copy-start.2 = (bf16[16,4608]{1,0:T(8,128)(2,1)S(1)}, bf16[16,4608]{1,0:T(8,128)(2,1)}, u32[]{:S(2)}) copy-start(bf16[16,4608]{1,0:T(8,128)(2,1)} %param.12) | copy-start | bytes 442372
  6.5 38.4 %all-gather.4.cloned.1.call-start = ((), (), s32[]{:S(2)}) async-start(), calls=%async_computation.1 | async-start | bytes 1310720 | tf_op jit(solution)/shard_map/all_gather | solution.py:39
  8.4 60.4 %all-gather.6.cloned.1.call-start = ((), (), s32[]{:S(2)}) async-start(), calls=%async_computation.2 | async-start | bytes 2949120 | tf_op jit(solution)/shard_map/all_gather | solution.py:20
  9.2 228.1 %all-gather.8.cloned.1.call-start = ((), (), s32[]{:S(2)}) async-start(), calls=%async_computation.3 | async-start | bytes 11796480 | tf_op jit(solution)/shard_map/all_gather | solution.py:33
  9.9 259.4 %reduce-scatter.2.cloned.1.call-start = ((), (), s32[]{:S(2)}) async-start(), calls=%async_computation.4 | async-start | bytes 327680 | tf_op jit(solution)/shard_map/reduce_scatter | solution.py:88
  10.0 238.3 %collective-permute-start.3 = (bf16[16,4608]{1,0:T(8,128)(2,1)S(1)}, bf16[16,4608]{1,0:T(8,128)(2,1)S(1)}, u32[]{:S(2)}, u32[]{:S(2)}) collective-permute-start(bf16[16,4608]{1,0:T(8,128)(2,1)S(1)} %copy-done.2), channel_id=1, source_target_pairs={{0,12},{4,0},{8,4},{12,8},{1,13},{5,1},{9,5},{13,9},{2,14},{6,2},{... | collective-permute-start | bytes 442376 | tf_op jit(solution)/shard_map/while/body/eval_jaxpr/ppermute | solution.py:10
  15.1 29.7 %collective-permute-start.1 = (bf16[16,4608]{1,0:T(8,128)(2,1)S(1)}, bf16[16,4608]{1,0:T(8,128)(2,1)S(1)}, u32[]{:S(2)}, u32[]{:S(2)}) collective-permute-start(bf16[16,4608]{1,0:T(8,128)(2,1)S(1)} %copy-done.2), channel_id=1, source_target_pairs={{0,4},{4,8},{8,12},{12,0},{1,5},{5,9},{9,13},{13,1},{2,6},{6,10},{... | collective-permute-start | bytes 442376 | tf_op jit(solution)/shard_map/while/body/eval_jaxpr/ppermute | solution.py:10
  22.6 7.2 %copy-start.3 = (s32[256]{0:T(256)S(1)}, s32[256]{0:T(256)}, u32[]{:S(2)}) copy-start(s32[256]{0:T(256)} %param.11) | copy-start | bytes 3076
  22.6 7.3 %copy-start.4 = (s32[256]{0:T(256)S(1)}, s32[256]{0:T(256)}, u32[]{:S(2)}) copy-start(s32[256]{0:T(256)} %param.13) | copy-start | bytes 3076
  22.6 7.5 %copy-start.5 = (s32[4,4]{1,0:T(4,128)S(1)}, s32[4,4]{1,0:T(4,128)}, u32[]{:S(2)}) copy-start(s32[4,4]{1,0:T(4,128)} %param.17) | copy-start | bytes 196
  26.0 13.0 %collective-permute-start.2 = (bf16[64,512]{1,0:T(8,128)(2,1)S(1)}, bf16[64,512]{1,0:T(8,128)(2,1)S(1)}, u32[]{:S(2)}, u32[]{:S(2)}) collective-permute-start(bf16[64,512]{1,0:T(8,128)(2,1)S(1)} %copy_bitcast_fusion), channel_id=1, source_target_pairs={{0,12},{4,0},{8,4},{12,8},{1,13},{5,1},{9,5},{13,9},{2,14},{6,2},{... | collective-permute-start | bytes 196616 | tf_op jit(solution)/shard_map/while/body/eval_jaxpr/ppermute | solution.py:10
  29.8 7.9 %collective-permute-start = (bf16[64,512]{1,0:T(8,128)(2,1)S(1)}, bf16[64,512]{1,0:T(8,128)(2,1)S(1)}, u32[]{:S(2)}, u32[]{:S(2)}) collective-permute-start(bf16[64,512]{1,0:T(8,128)(2,1)S(1)} %copy_bitcast_fusion), channel_id=1, source_target_pairs={{0,4},{4,8},{8,12},{12,0},{1,5},{5,9},{9,13},{13,1},{2,6},{6,10},{... | collective-permute-start | bytes 196616 | tf_op jit(solution)/shard_map/while/body/eval_jaxpr/ppermute | solution.py:10
  37.8 7.0 %collective-permute-start.4 = (bf16[64,512]{1,0:T(8,128)(2,1)S(1)}, bf16[64,512]{1,0:T(8,128)(2,1)S(1)}, u32[]{:S(2)}, u32[]{:S(2)}) collective-permute-start(bf16[64,512]{1,0:T(8,128)(2,1)S(1)} %collective-permute-done), channel_id=1, source_target_pairs={{0,4},{4,8},{8,12},{12,0},{1,5},{5,9},{9,13},{13,1},{2,6},{6,10},{... | collective-permute-start | bytes 196616 | tf_op jit(solution)/shard_map/ppermute | solution.py:10
  44.8 204.7 %collective-permute-start.5 = (bf16[16,4608]{1,0:T(8,128)(2,1)S(1)}, bf16[16,4608]{1,0:T(8,128)(2,1)S(1)}, u32[]{:S(2)}, u32[]{:S(2)}) collective-permute-start(bf16[16,4608]{1,0:T(8,128)(2,1)S(1)} %collective-permute-done.1), channel_id=1, source_target_pairs={{0,4},{4,8},{8,12},{12,0},{1,5},{5,9},{9,13},{13,1},{2,6},{6,10},{... | collective-permute-start | bytes 442376 | tf_op jit(solution)/shard_map/ppermute | solution.py:10
  244.5 1.8 copy-start
  250.3 0.7 copy-start.1
Sparse Core Ops, SparseCore 0:
  8.9 33.7 all-gather.3
  44.2 24.5 all-gather.5
  70.4 166.7 all-gather.7
  251.1 18.2 reduce-scatter.1
where the time goes:
time: 278 us; the launch traced here: 277 us
  waiting for transfers between devices  216 us (78%)
  between operations  16 us (6%)
  matrix products  14.3 us (5%)
  starting transfers between devices  10.4 us (4%)
  local copies, waits for them, and re-layouts  9.07 us (3%)
  blocking collectives  7.51 us (3%)
  other arithmetic  4.37 us (2%)
    all_gather x1, waiting for transfers between devices, shards(): lax.all_gather(out_proj, 'tgt', axis=1, tiled=True)  168 us
    reduce_scatter x1, waiting for transfers between devices, shards(): lax.psum_scatter(partial_value, 'src', scatter_dimension=0, tiled=True)  18.4 us
    all_gather x1, waiting for transfers between devices, shards(): lax.all_gather(target_rows, 'src', axis=0, tiled=True)  17.4 us
    ppermute x6, starting transfers between devices, passed_along(): return lax.ppermute(value, axis, pairs)  10.2 us
    ppermute x6, waiting for transfers between devices, passed_along(): return lax.ppermute(value, axis, pairs)  10.2 us
    all_gather x1, blocking collectives, shards(): lax.all_gather(decoder_rows, 'src', axis=0, tiled=True)  7.51 us
    dot_general x1, matrix products, shards(): jnp.einsum('td,hde->the', full_targets, lax.all_gather(out_proj, 'tgt', a...  6.99 us
  transfers between devices with their start and end apart: 10, of which 5 were waited for; matrix products, arithmetic and copies ran while one was open for 8% of the time, Pallas kernels for 0%

commit v1 on v0

--- a/solution.py
+++ b/solution.py
@@ -2,6 +2,22 @@
 import jax.numpy as jnp
 from jax import lax
 from jax.sharding import PartitionSpec as P
+
+
+def ring_product(x, axis, dim, product):
+    devices, index, rows = (lax.axis_size(axis), lax.axis_index(axis), x.shape[dim])
+    right = [(i, (i + 1) % devices) for i in range(devices)]
+    behind = [(i, (i - 1) % devices) for i in range(devices)]
+    halfway = devices // 2
+    from_left = from_right = x
+    total = product(x, index * rows)
+    for step in range(1, halfway + 1):
+        from_left = lax.ppermute(from_left, axis, right)
+        if step < devices - halfway:
+            from_right = lax.ppermute(from_right, axis, behind)
+            total = total + product(from_right, (index + step) % devices * rows)
+        total = total + product(from_left, (index - step) % devices * rows)
+    return total
 
 
 def passed_along(value, axis, steps):
@@ -27,11 +43,16 @@
     head_dim = out_proj.shape[2]
     groups_here = value_proj.shape[0]
     repeat = heads_here // groups_here
-    read_sum = jnp.einsum(
-        "td,hde->the",
-        full_targets,
-        lax.all_gather(out_proj, "tgt", axis=1, tiled=True),
-        preferred_element_type=jnp.float32,
+    read_sum = ring_product(
+        out_proj,
+        "tgt",
+        1,
+        lambda own_block_2, start: jnp.einsum(
+            "td,hde->the",
+            lax.dynamic_slice_in_dim(full_targets, start, own_block_2.shape[1], axis=1),
+            own_block_2,
+            preferred_element_type=jnp.float32,
+        ),
     )
     head_reads = read_sum.astype(jnp.bfloat16).reshape(tgt_dev, groups_here, repeat, head_dim)
     values = jnp.einsum("sd,gde->sge", full_sources, value_proj, preferred_element_type=jnp.float32)

time: 278 us -> 254 us (0.914)
  waiting for transfers between devices: 216 us -> 125 us
  starting transfers between devices: 10.4 us -> 63 us
  local copies, waits for them, and re-layouts: 9.07 us -> 15 us
  matrix products: 14.3 us -> 19.8 us
  other arithmetic: 4.37 us -> 7.33 us
    all_gather x1 -> x0, waiting for transfers between devices: 168 us -> none  [shards(): lax.all_gather(out_proj, 'tgt', axis=1, tiled=True)]
    ppermute x0 -> x3, starting transfers between devices: none -> 55.1 us  [the longest x2 52.4 us: ring_product(): from_left = lax.ppermute(from_left, axis, right)]
    ppermute x0 -> x3, waiting for transfers between devices: none -> 53.4 us  [the longest x2 53.4 us: ring_product(): from_left = lax.ppermute(from_left, axis, right)]
    ppermute x6, waiting for transfers between devices: 10.2 us -> 48.9 us  [passed_along(): return lax.ppermute(value, axis, pairs)]
    all_gather x1, waiting for transfers between devices: 17.4 us -> 0.01 us  [shards(): lax.all_gather(target_rows, 'src', axis=0, tiled=True)]
    reduce_scatter x1, waiting for transfers between devices: 18.4 us -> 22.4 us  [shards(): lax.psum_scatter(partial_value, 'src', scatter_dimension=0, tiled=True)]
    dot_general x4, matrix products: 2.81 us -> 6.47 us  [edge_tile(): jnp.einsum('sd,td->st', decoder_part, full_targets, preferred_element_typ...]
    gather x4, local copies, waits for them, and re-layouts: 2.38 us -> 5.46 us  [edge_tile(): weights = jnp.take(keyed_attn, key_positions, axis=1).astype(jnp.float32)]
  transfers between devices with their start and end apart: 10 -> 12, of which waited for: 5 -> 4; matrix products, arithmetic and copies ran while one was open for 8% -> 14% of each run, Pallas kernels for 0% -> 0%
where the time goes in v1:
time: 254 us
  waiting for transfers between devices  125 us (49%)
  starting transfers between devices  63 us (25%)
  matrix products  19.8 us (8%)
  between operations  16.1 us (6%)
  local copies, waits for them, and re-layouts  15 us (6%)
  blocking collectives  7.72 us (3%)
  other arithmetic  7.33 us (3%)
    ppermute x2, waiting for transfers between devices, ring_product(): from_left = lax.ppermute(from_left, axis, right)  53.4 us
    ppermute x2, starting transfers between devices, ring_product(): from_left = lax.ppermute(from_left, axis, right)  52.4 us
    ppermute x6, waiting for transfers between devices, passed_along(): return lax.ppermute(value, axis, pairs)  48.9 us
    reduce_scatter x1, waiting for transfers between devices, shards(): lax.psum_scatter(partial_value, 'src', scatter_dimension=0, tiled=True)  22.4 us
    dot_general x4, matrix products, shards(): jnp.einsum('td,hde->the', lax.dynamic_slice_in_dim(full_targets, start, o...  8.78 us
    ppermute x6, starting transfers between devices, passed_along(): return lax.ppermute(value, axis, pairs)  7.84 us
    all_gather x1, blocking collectives, shards(): lax.all_gather(decoder_rows, 'src', axis=0, tiled=True)  7.72 us
    dot_general x4, matrix products, edge_tile(): jnp.einsum('sd,td->st', decoder_part, full_targets, preferred_element_typ...  6.47 us
  transfers between devices with their start and end apart: 12, of which 4 were waited for; matrix products, arithmetic and copies ran while one was open for 14% of the time, Pallas kernels for 0%

profile of v1, /device:TPU:0, one launch (start us, length us, event | category | flops | bytes accessed | tf_op | source)
XLA Modules:
  0.0 253.8 jit_solution(5526496660185962488)
XLA Ops:
  6.5 1.8 copy.26
  8.4 0.0 all-gather.5.cloned.1.call-start
  8.5 3.1 %collective-permute-start.1 = (bf16[8,1152,128]{2,1,0:T(8,128)(2,1)}, bf16[8,1152,128]{2,1,0:T(8,128)(2,1)S(1)}, u32[]{:S(2)}, u32[]{:S(2)}) collective-permute-start(bf16[8,1152,128]{2,1,0:T(8,128)(2,1)} %param.14), channel_id=1, source_target_pairs={{0,4},{4,8},{8,12},{12,0},{1,5},{5,9},{9,13},{13,1},{2,6},{6,10},{... | collective-permute-start | bytes 7077896 | tf_op jit(solution)/shard_map/ppermute | solution.py:15
  11.6 0.0 reduce-scatter.2.cloned.1.call-start
  11.6 2.7 %collective-permute-start = (bf16[8,1152,128]{2,1,0:T(8,128)(2,1)}, bf16[8,1152,128]{2,1,0:T(8,128)(2,1)}, u32[]{:S(2)}, u32[]{:S(2)}) collective-permute-start(bf16[8,1152,128]{2,1,0:T(8,128)(2,1)} %param.14), channel_id=1, source_target_pairs={{0,12},{4,0},{8,4},{12,8},{1,13},{5,1},{9,5},{13,9},{2,14},{6,2},{... | collective-permute-start | bytes 7077896 | tf_op jit(solution)/shard_map/ppermute | solution.py:17
  14.3 7.7 %all_gather.11 = bf16[64,4608]{1,0:T(8,128)(2,1)S(1)} all-gather(bf16[16,4608]{1,0:T(8,128)(2,1)} %param.12), channel_id=1, replica_groups=mesh['grp'=2,'tgt'=4,'src'=4] {'src'}, dimensions={0}, use_global_device_ids=true | all-gather | bytes 737280 | tf_op jit(solution)/shard_map/all_gather | solution.py:37
  22.1 3.3 %convolution_convert_fusion = bf16[64,4,128]{2,0,1:T(8,128)(2,1)S(1)} fusion(bf16[4,4608,128]{2,1,0:T(8,128)(2,1)} %param.15, bf16[64,4608]{1,0:T(8,128)(2,1)S(1)} %all_gather.11), kind=kOutput, calls=%fused_computation.9 | convolution fusion | flops 302022656 | bytes 5373952 | tf_op jit(solution)/shard_map/sd,gde->sge/dot_general | solution.py:58
  25.4 1.0 collective-permute-start.3
  26.4 3.0 %collective-permute-start.5 = (bf16[64,512]{1,0:T(8,128)(2,1)S(1)}, bf16[64,512]{1,0:T(8,128)(2,1)S(1)}, u32[]{:S(2)}, u32[]{:S(2)}) collective-permute-start(bf16[64,512]{1,0:T(8,128)(2,1)S(1)} %copy_bitcast_fusion), channel_id=1, source_target_pairs={{0,12},{4,0},{8,4},{12,8},{1,13},{5,1},{9,5},{13,9},{2,14},{6,2},{... | collective-permute-start | bytes 196616 | tf_op jit(solution)/shard_map/while/body/eval_jaxpr/ppermute | solution.py:26
  29.4 53.4 %collective-permute-done.1 = bf16[8,1152,128]{2,1,0:T(8,128)(2,1)S(1)} collective-permute-done((bf16[8,1152,128]{2,1,0:T(8,128)(2,1)}, bf16[8,1152,128]{2,1,0:T(8,128)(2,1)S(1)}, u32[]{:S(2)}, u32[]{:S(2)}) %collective-permute-start.1) | collective-permute-done | bytes 2359328 | tf_op jit(solution)/shard_map/ppermute | solution.py:15
  82.8 49.3 %collective-permute-start.2 = (bf16[8,1152,128]{2,1,0:T(8,128)(2,1)S(1)}, bf16[8,1152,128]{2,1,0:T(8,128)(2,1)}, u32[]{:S(2)}, u32[]{:S(2)}) collective-permute-start(bf16[8,1152,128]{2,1,0:T(8,128)(2,1)S(1)} %collective-permute-done.1), channel_id=1, source_target_pairs={{0,4},{4,8},{8,12},{12,0},{1,5},{5,9},{9,13},{13,1},{2,6},{6,10},{... | collective-permute-start | bytes 7077896 | tf_op jit(solution)/shard_map/ppermute | solution.py:15
  132.1 0.7 compare_and_fusion
  132.8 0.6 pad_clamp_fusion
  133.4 0.5 compare_and_fusion.4
  133.9 0.7 fusion.35
  137.2 0.8 collective-permute-done.3
  138.0 2.1 collective-permute-start.7
  140.0 0.7 fusion.36
  140.7 1.8 collective-permute-start.6
  142.5 0.6 reshape.55
  143.2 48.1 %collective-permute-done.7 = bf16[64,512]{1,0:T(8,128)(2,1)S(1)} collective-permute-done((bf16[64,512]{1,0:T(8,128)(2,1)S(1)}, bf16[64,512]{1,0:T(8,128)(2,1)S(1)}, u32[]{:S(2)}, u32[]{:S(2)}) %collective-permute-start.7) | collective-permute-done | bytes 65568 | tf_op jit(solution)/shard_map/ppermute | solution.py:26
  191.3 0.6 reshape.57
  192.0 2.0 gather_fusion
  194.0 2.2 select_bitcast_fusion
  196.2 2.2 copy.27
  198.4 1.4 gather_fusion.4
  199.8 1.4 gather_fusion.3
  201.2 1.3 gather_fusion.2
  202.6 1.3 gather_fusion.1
  203.9 2.8 %fusion.13 = f32[256,8,128]{2,0,1:T(8,128)S(1)} fusion(bf16[8,1152,128]{2,1,0:T(8,128)(2,1)} %param.14, bf16[256,4608]{1,0:T(8,128)(2,1)} %all-gather.5.cloned.1.call-done, s32[]{:T(128)S(6)} %select_n.122), kind=kOutput, calls=%fused_computation.27 | convolution fusion | flops 603979776 | bytes 3997700 | tf_op jit(solution)/shard_map/td,hde->the/dot_general | solution.py:50
  206.7 2.5 convolution_add_fusion.2
  209.3 0.9 convolution_add_fusion.1
  210.2 2.6 %fusion = bf16[256,8,128]{2,0,1:T(8,128)(2,1)S(1)} fusion(f32[256,8,128]{2,0,1:T(8,128)S(1)} %convolution_add_fusion.1, bf16[8,1152,128]{2,1,0:T(8,128)(2,1)} %collective-permute-done.2, bf16[256,4608]{1,0:T(8,128)(2,1)S(1)} %copy-done, s32[]{:T(128)S(6)} %select_n.128), kind=kOutput, calls=%fused_computation.8 | convolution fusion | flops 604504064 | bytes 4521988 | tf_op jit(solution)/shard_map/td,hde->the/dot_general | solution.py:50
  212.8 0.3 fusion.23
  213.1 0.3 fusion.25
  213.4 0.3 fusion.27
  213.7 0.3 fusion.29
  214.0 0.4 fusion.21
  214.5 0.4 fusion.22
  215.0 1.6 fusion.8
  216.7 1.6 fusion.6
  218.4 0.4 fusion.20
  218.8 1.6 fusion.4
  220.5 0.4 fusion.19
  221.0 1.6 fusion.2
  222.6 0.7 copy-done.5
  223.4 22.4 %reduce-scatter.2.cloned.1.call-done = f32[64,256]{1,0:T(8,128)} async-done(((f32[256,256]{1,0:T(8,128)}), f32[64,256]{1,0:T(8,128)}) %reduce-scatter.2.cloned.1.call-update) | async-done | bytes 65552 | tf_op jit(solution)/shard_map/reduce_scatter | solution.py:109
  245.8 1.5 convert_element_type.69
  (62 shorter events, 0.4 us)
Async XLA Ops:
  6.5 185.4 %all-gather.3.cloned.1.call-start = ((), (), s32[]{:S(2)}) async-start(), calls=%async_computation.1 | async-start | bytes 1310720 | tf_op jit(solution)/shard_map/all_gather | solution.py:60
  8.4 195.5 %all-gather.5.cloned.1.call-start = ((), (), s32[]{:S(2)}) async-start(), calls=%async_computation.2 | async-start | bytes 2949120 | tf_op jit(solution)/shard_map/all_gather | solution.py:36
  8.5 74.3 %collective-permute-start.1 = (bf16[8,1152,128]{2,1,0:T(8,128)(2,1)}, bf16[8,1152,128]{2,1,0:T(8,128)(2,1)S(1)}, u32[]{:S(2)}, u32[]{:S(2)}) collective-permute-start(bf16[8,1152,128]{2,1,0:T(8,128)(2,1)} %param.14), channel_id=1, source_target_pairs={{0,4},{4,8},{8,12},{12,0},{1,5},{5,9},{9,13},{13,1},{2,6},{6,10},{... | collective-permute-start | bytes 7077896 | tf_op jit(solution)/shard_map/ppermute | solution.py:15
  11.6 234.2 %reduce-scatter.2.cloned.1.call-start = ((), (), s32[]{:S(2)}) async-start(), calls=%async_computation.3 | async-start | bytes 327680 | tf_op jit(solution)/shard_map/reduce_scatter | solution.py:109
  11.6 195.1 %collective-permute-start = (bf16[8,1152,128]{2,1,0:T(8,128)(2,1)}, bf16[8,1152,128]{2,1,0:T(8,128)(2,1)}, u32[]{:S(2)}, u32[]{:S(2)}) collective-permute-start(bf16[8,1152,128]{2,1,0:T(8,128)(2,1)} %param.14), channel_id=1, source_target_pairs={{0,12},{4,0},{8,4},{12,8},{1,13},{5,1},{9,5},{13,9},{2,14},{6,2},{... | collective-permute-start | bytes 7077896 | tf_op jit(solution)/shard_map/ppermute | solution.py:17
  14.3 177.6 %collective-permute-start.4 = (bf16[16,4608]{1,0:T(8,128)(2,1)}, bf16[16,4608]{1,0:T(8,128)(2,1)}, u32[]{:S(2)}, u32[]{:S(2)}) collective-permute-start(bf16[16,4608]{1,0:T(8,128)(2,1)} %param.12), channel_id=1, source_target_pairs={{0,4},{4,8},{8,12},{12,0},{1,5},{5,9},{9,13},{13,1},{2,6},{6,10},{... | collective-permute-start | bytes 442376 | tf_op jit(solution)/shard_map/while/body/eval_jaxpr/ppermute | solution.py:26
  22.1 110.0 %copy-start.8 = (s32[256]{0:T(256)S(1)}, s32[256]{0:T(256)}, u32[]{:S(2)}) copy-start(s32[256]{0:T(256)} %param.11) | copy-start | bytes 3076
  22.1 110.0 %copy-start.9 = (s32[256]{0:T(256)S(1)}, s32[256]{0:T(256)}, u32[]{:S(2)}) copy-start(s32[256]{0:T(256)} %param.13) | copy-start | bytes 3076
  22.1 111.8 %copy-start.14 = (s32[4,4]{1,0:T(4,128)S(1)}, s32[4,4]{1,0:T(4,128)}, u32[]{:S(2)}) copy-start(s32[4,4]{1,0:T(4,128)} %param.17) | copy-start | bytes 196
  25.4 112.6 %collective-permute-start.3 = (bf16[64,512]{1,0:T(8,128)(2,1)S(1)}, bf16[64,512]{1,0:T(8,128)(2,1)S(1)}, u32[]{:S(2)}, u32[]{:S(2)}) collective-permute-start(bf16[64,512]{1,0:T(8,128)(2,1)S(1)} %copy_bitcast_fusion), channel_id=1, source_target_pairs={{0,4},{4,8},{8,12},{12,0},{1,5},{5,9},{9,13},{13,1},{2,6},{6,10},{... | collective-permute-start | bytes 196616 | tf_op jit(solution)/shard_map/while/body/eval_jaxpr/ppermute | solution.py:26
  26.4 114.3 %collective-permute-start.5 = (bf16[64,512]{1,0:T(8,128)(2,1)S(1)}, bf16[64,512]{1,0:T(8,128)(2,1)S(1)}, u32[]{:S(2)}, u32[]{:S(2)}) collective-permute-start(bf16[64,512]{1,0:T(8,128)(2,1)S(1)} %copy_bitcast_fusion), channel_id=1, source_target_pairs={{0,12},{4,0},{8,4},{12,8},{1,13},{5,1},{9,5},{13,9},{2,14},{6,2},{... | collective-permute-start | bytes 196616 | tf_op jit(solution)/shard_map/while/body/eval_jaxpr/ppermute | solution.py:26
  82.8 127.4 %collective-permute-start.2 = (bf16[8,1152,128]{2,1,0:T(8,128)(2,1)S(1)}, bf16[8,1152,128]{2,1,0:T(8,128)(2,1)}, u32[]{:S(2)}, u32[]{:S(2)}) collective-permute-start(bf16[8,1152,128]{2,1,0:T(8,128)(2,1)S(1)} %collective-permute-done.1), channel_id=1, source_target_pairs={{0,4},{4,8},{8,12},{12,0},{1,5},{5,9},{9,13},{13,1},{2,6},{6,10},{... | collective-permute-start | bytes 7077896 | tf_op jit(solution)/shard_map/ppermute | solution.py:15
  138.0 53.4 %collective-permute-start.7 = (bf16[64,512]{1,0:T(8,128)(2,1)S(1)}, bf16[64,512]{1,0:T(8,128)(2,1)S(1)}, u32[]{:S(2)}, u32[]{:S(2)}) collective-permute-start(bf16[64,512]{1,0:T(8,128)(2,1)S(1)} %collective-permute-done.3), channel_id=1, source_target_pairs={{0,4},{4,8},{8,12},{12,0},{1,5},{5,9},{9,13},{13,1},{2,6},{6,10},{... | collective-permute-start | bytes 196616 | tf_op jit(solution)/shard_map/ppermute | solution.py:26
  140.7 78.1 %collective-permute-start.6 = (bf16[16,4608]{1,0:T(8,128)(2,1)}, bf16[16,4608]{1,0:T(8,128)(2,1)}, u32[]{:S(2)}, u32[]{:S(2)}) collective-permute-start(bf16[16,4608]{1,0:T(8,128)(2,1)} %param.12), channel_id=1, source_target_pairs={{0,12},{4,0},{8,4},{12,8},{1,13},{5,1},{9,5},{13,9},{2,14},{6,2},{... | collective-permute-start | bytes 442376 | tf_op jit(solution)/shard_map/while/body/eval_jaxpr/ppermute | solution.py:26
  192.0 29.0 %collective-permute-start.8 = (bf16[16,4608]{1,0:T(8,128)(2,1)}, bf16[16,4608]{1,0:T(8,128)(2,1)}, u32[]{:S(2)}, u32[]{:S(2)}) collective-permute-start(bf16[16,4608]{1,0:T(8,128)(2,1)} %collective-permute-done.4), channel_id=1, source_target_pairs={{0,4},{4,8},{8,12},{12,0},{1,5},{5,9},{9,13},{13,1},{2,6},{6,10},{... | collective-permute-start | bytes 442376 | tf_op jit(solution)/shard_map/ppermute | solution.py:26
  203.9 2.9 %copy-start = (bf16[256,4608]{1,0:T(8,128)(2,1)S(1)}, bf16[256,4608]{1,0:T(8,128)(2,1)}, u32[]{:S(2)}) copy-start(bf16[256,4608]{1,0:T(8,128)(2,1)} %all-gather.5.cloned.1.call-done) | copy-start | bytes 7077892
  210.1 2.9 %copy-start.7 = (bf16[64,4,128]{2,1,0:T(4,128)(2,1)S(1)}, bf16[64,4,128]{2,1,0:T(4,128)(2,1)}, u32[]{:S(2)}) copy-start(bf16[64,4,128]{2,1,0:T(4,128)(2,1)} %reshape.57) | copy-start | bytes 196612
  210.1 3.3 %copy-start.6 = (bf16[64,4,128]{2,1,0:T(4,128)(2,1)S(1)}, bf16[64,4,128]{2,1,0:T(4,128)(2,1)}, u32[]{:S(2)}) copy-start(bf16[64,4,128]{2,1,0:T(4,128)(2,1)} %reshape.55) | copy-start | bytes 196612
  212.7 1.3 copy-start.4
  212.7 1.3 copy-start.13
  213.1 1.4 copy-start.3
  213.1 1.4 copy-start.12
  213.1 1.9 copy-start.18
  214.0 2.7 %copy-start.17 = (s32[16]{0:T(128)S(1)}, s32[16]{0:T(128)}, u32[]{:S(2)}) copy-start(s32[16]{0:T(128)} %get-tuple-element.65) | copy-start | bytes 196
  214.9 3.4 %copy-start.2 = (bf16[64,8,256]{2,1,0:T(8,128)(2,1)S(1)}, bf16[64,8,256]{2,1,0:T(8,128)(2,1)}, u32[]{:S(2)}) copy-start(bf16[64,8,256]{2,1,0:T(8,128)(2,1)} %gather_fusion.3) | copy-start | bytes 786436
  214.9 3.4 %copy-start.11 = (pred[64]{0:T(512)(128)(4,1)S(1)}, pred[64]{0:T(512)(128)(4,1)}, u32[]{:S(2)}) copy-start(pred[64]{0:T(512)(128)(4,1)} %get-tuple-element.67) | copy-start | bytes 196
  216.6 2.2 copy-start.16
  218.3 2.2 copy-start.1
  218.3 2.2 copy-start.10
  218.3 2.6 %copy-start.15 = (s32[16]{0:T(128)S(1)}, s32[16]{0:T(128)}, u32[]{:S(2)}) copy-start(s32[16]{0:T(128)} %get-tuple-element.62) | copy-start | bytes 196
  222.6 0.7 copy-start.5
Sparse Core Ops, SparseCore 0:
  8.9 81.8 all-gather.2
  92.3 22.7 all-gather.4
  223.5 22.2 reduce-scatter.1
